TPU v7x, 256 devices: a whole 4x4x8 slice. The times are simulated.
256 devices in a mesh: chan: 128 (over z, x, y_hi, core), rng: 2 (over y_lo).
Axes of the slice: x: 4, y: 4 (y_hi: 2, y_lo: 2; y = y_hi * 2 + y_lo), z: 8, core: 2. Of those that a mesh axis runs over, the one named last changes fastest.
Arguments:
- radar_cube: bfloat16 [2, 4096, 64, 256], P(None, 'chan', None, 'rng'), may hold values from -31 to 31, as said below
- offsets: int32 [256], P('chan'), may hold values from 0 to 7
- train_index: int32 [128], P('rng'), may hold values from 0 to 127, as said below
- guard_mask: int32 [256], P('rng'), may hold values 0 or 1
- weights: bfloat16 [2, 256, 64, 96], P(None, 'chan'), may hold values from -0.625 to 0.625
Outputs:
- covariance: float32 [64, 256, 2, 9216], P('rng', 'chan')
- matched_stat: float32 [256, 64, 256], P('chan', None, 'rng')
- power_map: float32 [256, 64, 256], P('chan', None, 'rng')
Inputs may be any that keep to these rules, and one draw needn't show every extreme that they name: `radar_cube`: samples are finite real numbers. `weights`: for every subarray and bin, at least one of the 96 complex weights is nonzero. `train_index`: each aligned block of 64 entries lists distinct gates of the matching block of 128 gates, counted from that block's first gate.
All inputs are finite; a program needn't handle non-finite values. No bound on the sum of `guard_mask` on one device may be relied on, other than what follows from the above.
Results may differ from a plain program's by a relative error of at most 0.0039.
Values may be sent and summed in bfloat16 or wider, within the bound.
A program may use at most 128 MiB of HBM per device.

v0:
```python
import functools
import math

import jax
import jax.numpy as jnp
import numpy as np
from jax import lax
from jax.experimental import pallas as pl
from jax.experimental.pallas import tpu as pltpu
from jax.sharding import PartitionSpec as P

MESH = pl.DeviceIdType.MESH
F32 = jnp.float32
BF16 = jnp.bfloat16

PULSES = 64
CH = 32
SUB = 32
HALO = 24
EXT = CH + HALO
GATES = 128
TRAIN = 64
HALF = 32
BINS = HALF + 2
SLOTS = PULSES + 2
GROUP = 6
CHUNK = 4
N_CHUNK = HALF // CHUNK
ROWS = 144


def dft_matrix():
    freq = np.arange(PULSES)
    angle = (freq[:, None] * freq[None, :] % PULSES) * (2.0 * math.pi / PULSES)
    cosine = np.cos(angle) / math.sqrt(PULSES)
    sine = np.sin(angle) / math.sqrt(PULSES)
    return np.block([[cosine, sine], [-sine, cosine]]).astype(jnp.bfloat16)


def dot(a, b):
    return jnp.dot(a, b, preferred_element_type=F32)


def dot_nt(a, b):
    return lax.dot_general(a, b, (((1,), (1,)), ((), ())), preferred_element_type=F32)


def turned_by(x, shift):
    return pltpu.roll(x, shift % x.shape[0], 0) if shift else x


def kernel(
    sizes,
    off_ref,
    cube_hbm,
    idx_ref,
    guard_ref,
    wts_ref,
    dft_ref,
    cov_hbm,
    matched_ref,
    pmap_ref,
    cube,
    spec,
    bins_a,
    bins_b,
    train,
    train_halo,
    got_train,
    got_halo,
    send_wts,
    got_wts,
    lhs,
    filt_re,
    filt_im,
    send_part,
    got_part,
    send_quad,
    got_quad,
    sum_a,
    sum_b,
    ext_a,
    ext_b,
    rhs_re,
    rhs_im,
    lhs_cov,
    cov,
    cube_sem,
    cov_sem,
    send_sem,
    recv_sem,
    a_send,
    a_recv,
    b_send,
    b_recv,
):
    n_z, n_xy, n_chan, n_rng = sizes
    n_a, n_b = n_xy * n_rng, n_z * 2
    chan, rng = lax.axis_index("chan"), lax.axis_index("rng")
    other = 1 - rng
    prev, following = lax.rem(chan + n_chan - 1, n_chan), lax.rem(chan + 1, n_chan)
    core = lax.rem(chan, 2)
    chip = chan // 2
    z, xy = chip // n_xy, lax.rem(chip, n_xy)
    my_a, my_b = xy * n_rng + rng, z * 2 + core

    def peer_a(step):
        slot = lax.rem(my_a + step, n_a)
        return slot, ((z * n_xy + slot // n_rng) * 2 + core, lax.rem(slot, n_rng))

    def peer_b(step):
        slot = lax.rem(my_b + step, n_b)
        return slot, (((slot // 2) * n_xy + xy) * 2 + lax.rem(slot, 2), rng)

    def remote(src, dst, k, device):
        return pltpu.make_async_remote_copy(
            src_ref=src,
            dst_ref=dst,
            send_sem=send_sem.at[k],
            recv_sem=recv_sem.at[k],
            device_id=device,
            device_id_type=MESH,
        )

    fetch = pltpu.make_async_copy(cube_hbm, cube, cube_sem)
    fetch.start()
    barrier = pltpu.get_barrier_semaphore()
    for device in ((prev, rng), (following, rng), (prev, other), (following, other)):
        pl.semaphore_signal(barrier, inc=1, device_id=device, device_id_type=MESH)

    def greet_a(step, carry):
        pl.semaphore_signal(barrier, inc=1, device_id=peer_a(step)[1], device_id_type=MESH)
        return carry

    def greet_b(step, carry):
        pl.semaphore_signal(barrier, inc=1, device_id=peer_b(step)[1], device_id_type=MESH)
        return carry

    lax.fori_loop(1, n_a, greet_a, 0)
    lax.fori_loop(1, n_b, greet_b, 0)

    lane = lax.broadcasted_iota(jnp.int32, (1, 128), 1)
    depth = lax.broadcasted_iota(jnp.int32, (96, 128), 0)
    placed = [[jnp.zeros((PULSES, 128), F32) for _ in range(3)] for _ in range(2)]
    for sub in range(2):
        for part in range(2):
            value = wts_ref[part, sub]
            for ahead in range(2):
                at = lax.rem(lane, 32) + (32 * ahead - 16 * sub) - off_ref[sub]
                fits = (at >= 0) & (at < SUB) & (lane // 32 == sub * 2 + part)
                for b in range(3):
                    hot = jnp.where(depth == jnp.where(fits, at + b * SUB, -1), 1.0, 0.0).astype(BF16)
                    placed[ahead][b] = placed[ahead][b] + dot(value, hot)
    for b in range(3):
        send_wts[b] = turned_by(placed[1][b], b - 1).astype(BF16)

    def fill_lhs(tables):
        for b in range(3):
            lhs[pl.ds(b * 2, PULSES, stride=8), :] = tables[b]
            lhs[pl.ds(b * 2 + 1, PULSES, stride=8), :] = pltpu.roll(tables[b], 64, 1)

    gate = lax.broadcasted_iota(jnp.int32, (GATES, 128), 0)
    wanted = jnp.concatenate([idx_ref[...], idx_ref[...]], axis=1)
    hits = jnp.where(gate == wanted, 1.0, 0.0)
    guard = jnp.broadcast_to(guard_ref[...].astype(F32), (8, GATES)).astype(BF16)
    keep = dot(guard, hits.astype(BF16))[0:1]
    pick = (hits * keep).astype(BF16)
    counts = dot_nt(jnp.full((8, 128), 0.5, BF16), pick)[0:1]

    pl.semaphore_wait(barrier, 4 + (n_a - 1) + (n_b - 1))
    wts_copy = remote(send_wts, got_wts, 0, (following, rng))
    wts_copy.start()
    fill_lhs([turned_by(placed[0][b], b - 1) for b in range(3)])

    fetch.wait()
    table = dft_ref[...]

    def doppler(step, carry):
        for u in range(2):
            m = step * 4 + 2 * u
            pair = [jnp.concatenate([cube[0, m + v], cube[1, m + v]], axis=0) for v in range(2)]
            out = dot(table, jnp.concatenate(pair, axis=1))
            for v in range(2):
                for part in range(2):
                    start = pl.multiple_of((part * CH + m + v) * PULSES, PULSES)
                    spec[pl.ds(start, PULSES), :] = out[part * 64 : part * 64 + 64, v * 128 : v * 128 + 128]
        return carry

    lax.fori_loop(0, CH // 4, doppler, 0)

    left = lax.broadcasted_iota(jnp.int32, (CH, 128), 1) < TRAIN

    def per_bin(step, carry):
        rows = []
        for u in range(GROUP):
            k = lax.rem(step * GROUP + u + PULSES - 1, PULSES)
            re = spec[pl.ds(k, CH, stride=PULSES), :]
            im = spec[pl.ds(k + CH * PULSES, CH, stride=PULSES), :]
            both = jnp.concatenate([re, im], axis=0).astype(BF16)
            bins_a[k] = both
            bins_b[k] = jnp.concatenate([im, -re], axis=0).astype(BF16)
            rows.append(both)
        chosen = dot(jnp.concatenate(rows, axis=0), pick)
        tiles = []
        for u in range(GROUP):
            tile = jnp.where(left, chosen[u * 64 : u * 64 + 32], chosen[u * 64 + 32 : u * 64 + 64])
            train[step * GROUP + u] = tile.astype(BF16)
            tiles.append(tile[:HALO])
        start = pl.multiple_of(step * (GROUP * HALO), GROUP * HALO)
        train_halo[pl.ds(start, GROUP * HALO), :] = jnp.concatenate(tiles, axis=0).astype(BF16)
        return carry

    lax.fori_loop(0, SLOTS // GROUP, per_bin, 0)

    halo_rows = BINS * HALO
    train_copy = remote(train.at[pl.ds(other * HALF, BINS)], got_train, 1, (chan, other))
    same_copy = remote(
        train_halo.at[pl.ds(pl.multiple_of(rng * (HALF * HALO), HALF * HALO), halo_rows)], got_halo.at[0], 2, (prev, rng)
    )
    cross_copy = remote(
        train_halo.at[pl.ds(pl.multiple_of(other * (HALF * HALO), HALF * HALO), halo_rows)], got_halo.at[1], 3, (prev, other)
    )
    train_copy.start()
    same_copy.start()
    cross_copy.start()

    def filtered():
        def one(step, carry):
            for u in range(8):
                k = step * 8 + u
                row = pl.multiple_of(k * 8, 8)
                weight = lhs[pl.ds(row, 8), :][:, :64].astype(BF16)
                out = dot(weight, jnp.concatenate([bins_a[k], bins_b[k]], axis=1))
                filt_re[pl.ds(row, 8), :] = out[:, :128]
                filt_im[pl.ds(row, 8), :] = out[:, 128:]
            return carry

        lax.fori_loop(0, PULSES // 8, one, 0)
        sums = []
        for sub in range(2):
            for ref in (filt_re, filt_im):
                terms = [turned_by(ref[pl.ds(b * 2 + sub, PULSES, stride=8), :], 1 - b) for b in range(3)]
                sums.append(terms[0] + terms[1] + terms[2])
        return sums

    own = filtered()
    wts_copy.wait()
    fill_lhs([got_wts[b].astype(F32) for b in range(3)])
    for part, value in enumerate(filtered()):
        send_part[part] = value
    part_copy = remote(send_part, got_part, 4, (prev, rng))
    part_copy.start()

    norms = []
    for sub in range(2):
        re, im = wts_ref[0, sub].astype(F32), wts_ref[1, sub].astype(F32)
        norms.append(jnp.sum(re * re + im * im, axis=1, keepdims=True))

    def own_rows(k, carry):
        start = pl.multiple_of(k * EXT, 8)
        ext_a[pl.ds(start, CH), :] = train[rng * HALF + k].astype(F32)
        return carry

    lax.fori_loop(0, BINS, own_rows, 0)

    part_copy.wait()
    powers = []
    for sub in range(2):
        re = own[2 * sub] + got_part[2 * sub]
        im = own[2 * sub + 1] + got_part[2 * sub + 1]
        powers.append(re * re + im * im)
    quads = [jnp.sum(p * counts, axis=1, keepdims=True) for p in powers]
    send_quad[...] = jnp.where(lane < 64, quads[0], quads[1])
    quad_copy = remote(send_quad, got_quad, 5, (chan, other))
    quad_copy.start()
    sum_a[my_a] = jnp.sum(powers[0] + powers[1], axis=0, keepdims=True)

    def copy_a(step):
        return pltpu.make_async_remote_copy(
            src_ref=sum_a.at[my_a],
            dst_ref=sum_a.at[my_a],
            send_sem=a_send.at[step],
            recv_sem=a_recv.at[my_a],
            device_id=peer_a(step)[1],
            device_id_type=MESH,
        )

    def copy_b(step):
        return pltpu.make_async_remote_copy(
            src_ref=sum_b.at[my_b],
            dst_ref=sum_b.at[my_b],
            send_sem=b_send.at[step],
            recv_sem=b_recv.at[my_b],
            device_id=peer_b(step)[1],
            device_id_type=MESH,
        )

    def start_a(step, carry):
        copy_a(step).start()
        return carry

    def start_b(step, carry):
        copy_b(step).start()
        return carry

    def finish_a(step, carry):
        slot, device = peer_a(step)
        pltpu.make_async_remote_copy(
            src_ref=sum_a.at[my_a],
            dst_ref=sum_a.at[slot],
            send_sem=a_send.at[step],
            recv_sem=a_recv.at[slot],
            device_id=device,
            device_id_type=MESH,
        ).wait()
        return carry

    def finish_b(step, carry):
        slot, device = peer_b(step)
        pltpu.make_async_remote_copy(
            src_ref=sum_b.at[my_b],
            dst_ref=sum_b.at[slot],
            send_sem=b_send.at[step],
            recv_sem=b_recv.at[slot],
            device_id=device,
            device_id_type=MESH,
        ).wait()
        return carry

    lax.fori_loop(1, n_a, start_a, 0)

    train_copy.wait()
    same_copy.wait()
    cross_copy.wait()
    low = lax.broadcasted_iota(jnp.int32, (SUB, 128), 1) < TRAIN

    def windows(k, carry):
        start = pl.multiple_of(k * EXT, 8)
        ext_b[pl.ds(start, CH), :] = got_train[k].astype(F32)
        return carry

    lax.fori_loop(0, BINS, windows, 0)

    def halos(step, carry):
        rows = pl.multiple_of(step * (2 * HALO), 2 * HALO)
        for ext, which in ((ext_a, 0), (ext_b, 1)):
            pair = got_halo[which, pl.ds(rows, 2 * HALO), :].astype(F32)
            for u in range(2):
                start = pl.multiple_of((step * 2 + u) * EXT + CH, 8)
                ext[pl.ds(start, HALO), :] = pair[u * HALO : u * HALO + HALO]
        return carry

    lax.fori_loop(0, BINS // 2, halos, 0)

    def arrange(k, carry):
        row = pl.multiple_of(k * SUB, SUB)
        for sub in range(2):
            start = k * EXT + 16 * sub + off_ref[sub]
            natural = [ext[pl.ds(start, SUB), :] for ext in (ext_a, ext_b)]
            turned = [pltpu.roll(x, 64, 1) for x in natural]
            rhs_re[sub, pl.ds(row, SUB), :] = jnp.concatenate(natural, axis=1).astype(BF16)
            rhs_im[sub, pl.ds(row, SUB), :] = jnp.concatenate([jnp.where(low, -x, x) for x in turned], axis=1).astype(BF16)
            by_four = [
                jnp.concatenate([ext[pl.ds(start + a, 8, stride=4), :] for a in range(4)], axis=0)
                for ext in (ext_a, ext_b)
            ]
            lhs_cov[sub, pl.ds(row, SUB), :] = jnp.concatenate(by_four, axis=1).astype(BF16)
        return carry

    lax.fori_loop(0, BINS, arrange, 0)

    col = lax.broadcasted_iota(jnp.int32, (24, 128), 1)

    def one_bin(k, carry):
        row = pl.multiple_of(k * SUB, SUB)
        for sub in range(2):
            left_rows = lhs_cov[sub, pl.ds(row, 96), :]
            right = jnp.concatenate([rhs_re[sub, pl.ds(row, 128), :], rhs_im[sub, pl.ds(row, 128), :]], axis=0)
            out = dot_nt(left_rows, right) * (1.0 / 128.0)
            base = (k * 2 + sub) * ROWS
            for part in range(2):
                half = out[:, part * 128 : part * 128 + 128]
                by = [
                    jnp.concatenate([half[b * 32 + a * 8 : b * 32 + a * 8 + 8] for b in range(3)], axis=0)
                    for a in range(4)
                ]
                r1, r2, r3 = pltpu.roll(by[1], 96, 1), pltpu.roll(by[2], 64, 1), pltpu.roll(by[3], 32, 1)
                cov[pl.ds(base + part, 24, stride=6), :] = jnp.where(col < 96, by[0], r1)
                cov[pl.ds(base + 2 + part, 24, stride=6), :] = jnp.where(col < 64, r1, r2)
                cov[pl.ds(base + 4 + part, 24, stride=6), :] = jnp.where(col < 32, r2, r3)
        return carry

    def cov_copy(chunk):
        rows = pl.ds(pl.multiple_of(chunk * (CHUNK * 2 * ROWS), CHUNK * 2 * ROWS), CHUNK * 2 * ROWS)
        return pltpu.make_async_copy(cov.at[rows], cov_hbm.at[rows], cov_sem.at[chunk])

    def one_chunk(chunk, carry):
        lax.fori_loop(chunk * CHUNK, chunk * CHUNK + CHUNK, one_bin, 0)
        cov_copy(chunk).start()
        return carry

    def chunk_done(chunk, carry):
        cov_copy(chunk).wait()
        return carry

    lax.fori_loop(0, N_CHUNK // 2, one_chunk, 0)

    lax.fori_loop(1, n_a, finish_a, 0)
    sum_b[my_b] = jnp.sum(sum_a[...], axis=0)
    lax.fori_loop(1, n_b, start_b, 0)
    lax.fori_loop(N_CHUNK // 2, N_CHUNK, one_chunk, 0)

    quad_copy.wait()
    quad_sum = send_quad[...] + got_quad[...]
    for sub in range(2):
        quad = quad_sum[:, sub * 64 : sub * 64 + 1] * (1.0 / 128.0) + norms[sub]
        matched_ref[sub] = powers[sub] / quad

    lax.fori_loop(1, n_b, finish_b, 0)
    total = jnp.sum(jnp.sum(sum_b[...], axis=0), axis=1, keepdims=True)
    mean = total * (1.0 / (n_chan * n_rng * 2 * PULSES * GATES)) + 1e-6
    for sub in range(2):
        pmap_ref[sub] = powers[sub] / mean
    lax.fori_loop(0, N_CHUNK, chunk_done, 0)


def local(sizes, radar_cube, offsets, train_index, guard_mask, weights):
    n_z, n_xy, n_chan, n_rng = sizes
    n_a, n_b = n_xy * n_rng, n_z * 2
    dma = pltpu.SemaphoreType.DMA
    vmem = pl.BlockSpec(memory_space=pltpu.VMEM)
    rows = HALF * 2 * ROWS
    cov, matched, pmap = pl.pallas_call(
        functools.partial(kernel, sizes),
        out_shape=(
            jax.ShapeDtypeStruct((rows, 128), F32),
            jax.ShapeDtypeStruct((2, PULSES, GATES), F32),
            jax.ShapeDtypeStruct((2, PULSES, GATES), F32),
        ),
        in_specs=[
            pl.BlockSpec(memory_space=pltpu.SMEM),
            pl.BlockSpec(memory_space=pl.ANY),
            vmem,
            vmem,
            vmem,
            vmem,
        ],
        out_specs=(pl.BlockSpec(memory_space=pl.ANY), vmem, vmem),
        scratch_shapes=[
            pltpu.VMEM((2, CH, PULSES, GATES), BF16),
            pltpu.VMEM((2 * CH * PULSES, GATES), F32),
            pltpu.VMEM((PULSES, 2 * CH, GATES), BF16),
            pltpu.VMEM((PULSES, 2 * CH, GATES), BF16),
            pltpu.VMEM((SLOTS, CH, 128), BF16),
            pltpu.VMEM((SLOTS * HALO, 128), BF16),
            pltpu.VMEM((BINS, CH, 128), BF16),
            pltpu.VMEM((2, BINS * HALO, 128), BF16),
            pltpu.VMEM((3, PULSES, 128), BF16),
            pltpu.VMEM((3, PULSES, 128), BF16),
            pltpu.VMEM((PULSES * 8, 128), F32),
            pltpu.VMEM((PULSES * 8, 128), F32),
            pltpu.VMEM((PULSES * 8, 128), F32),
            pltpu.VMEM((4, PULSES, GATES), F32),
            pltpu.VMEM((4, PULSES, GATES), F32),
            pltpu.VMEM((PULSES, 128), F32),
            pltpu.VMEM((PULSES, 128), F32),
            pltpu.VMEM((n_a, 1, 128), F32),
            pltpu.VMEM((n_b, 1, 128), F32),
            pltpu.VMEM((BINS * EXT, 128), F32),
            pltpu.VMEM((BINS * EXT, 128), F32),
            pltpu.VMEM((2, (BINS + 1) * SUB, 256), BF16),
            pltpu.VMEM((2, (BINS + 1) * SUB, 256), BF16),
            pltpu.VMEM((2, (BINS + 1) * SUB, 256), BF16),
            pltpu.VMEM((rows, 128), F32),
            dma,
            dma((N_CHUNK,)),
            dma((6,)),
            dma((6,)),
            dma((n_a,)),
            dma((n_a,)),
            dma((n_b,)),
            dma((n_b,)),
        ],
        compiler_params=pltpu.CompilerParams(collective_id=0, has_side_effects=True),
    )(
        offsets,
        radar_cube,
        train_index.reshape(1, -1),
        guard_mask.reshape(1, -1),
        weights,
        jnp.asarray(dft_matrix()),
    )
    cov = cov.reshape(HALF, 2, ROWS // 2, 2, 128).transpose(0, 1, 3, 2, 4).reshape(HALF, 2, 2, ROWS * 64)
    return cov, matched, pmap


def solution(mesh):
    n_chan, n_rng = mesh.shape["chan"], mesh.shape["rng"]
    n_xy = 8 if n_chan >= 64 else 2
    sizes = (n_chan // (2 * n_xy), n_xy, n_chan, n_rng)
    return jax.shard_map(
        functools.partial(local, sizes),
        mesh=mesh,
        in_specs=(
            P(None, "chan", None, "rng"),
            P("chan"),
            P("rng"),
            P("rng"),
            P(None, "chan", None, None),
        ),
        out_specs=(P("rng", "chan", None, None), P("chan", None, "rng"), P("chan", None, "rng")),
        check_vma=False,
    )
```

profile of v0, /device:TPU:1, one launch (start us, length us, event | category | flops | bytes accessed | tf_op | source)
XLA Modules:
  0.0 54.1 jit_solution(8906278956877897598)
XLA Ops:
  0.6 47.3 %shard_map.85 = (f32[9216,128]{1,0:T(8,128)}, f32[2,64,128]{2,1,0:T(8,128)}, f32[2,64,128]{2,1,0:T(8,128)}) custom-call(s32[2]{0:T(128)} %off_ref.1, bf16[2,32,64,128]{3,2,1,0:T(8,128)(2,1)} %cube_hbm.1, s32[1,64]{1,0:T(1,128)} %bitcast.8, s32[1,128]{1,0:T(1,128)} %bitcast.9, bf16[2,2,64,96]{3,2,1,0:T(8,128)(2,1)} %wts_ref.1, ...), custom_call_target="tpu_custom_call" | custom-call | tf_op jit(solution)/shard_map/pallas_call | solution.py:433
  47.9 0.0 copy-start.1
  47.9 0.0 copy-start
  47.9 4.9 %copy.13 = f32[32,2,2,9216]{3,2,1,0:T(2,128)} copy(f32[32,2,2,9216]{3,2,1,0:T(2,128)} %bitcast.7) | data formatting | bytes 9437184
  52.8 0.0 copy-done.1
  52.8 0.6 %copy.14 = f32[2,64,128]{2,1,0:T(8,128)} copy(f32[2,64,128]{2,1,0:T(8,128)S(1)} %copy-done.1) | data formatting | bytes 131072
  53.4 0.0 copy-done
  53.4 0.6 %copy.15 = f32[2,64,128]{2,1,0:T(8,128)} copy(f32[2,64,128]{2,1,0:T(8,128)S(1)} %copy-done) | data formatting | bytes 131072
Async XLA Ops:
  47.9 4.9 %copy-start.1 = (f32[2,64,128]{2,1,0:T(8,128)S(1)}, f32[2,64,128]{2,1,0:T(8,128)}, u32[]{:S(2)}) copy-start(f32[2,64,128]{2,1,0:T(8,128)} %get-tuple-element.13) | copy-start | bytes 196612
  47.9 5.5 %copy-start = (f32[2,64,128]{2,1,0:T(8,128)S(1)}, f32[2,64,128]{2,1,0:T(8,128)}, u32[]{:S(2)}) copy-start(f32[2,64,128]{2,1,0:T(8,128)} %get-tuple-element.14) | copy-start | bytes 196612
where the time goes:
time: 54.2 us; the launch traced here: 54.1 us
  Pallas kernels  47.3 us (87%)
  local copies, waits for them, and re-layouts  6.14 us (11%)
  between operations  0.66 us (1%)
    pallas_call x1, Pallas kernels, local(): pl.pallas_call(functools.partial(kernel, sizes), out_shape=(jax.ShapeDtyp...  47.3 us
    unnamed x7, local copies, waits for them, and re-layouts  6.14 us

commit v1 on v0

v1 whole, which is shorter than its diff:
```python
import functools
import math

import jax
import jax.numpy as jnp
import numpy as np
from jax import lax
from jax.experimental import pallas as pl
from jax.experimental.pallas import tpu as pltpu
from jax.sharding import PartitionSpec as P

MESH = pl.DeviceIdType.MESH
F32 = jnp.float32
BF16 = jnp.bfloat16

PULSES = 64
CH = 32
SUB = 32
HALO = 24
EXT = CH + HALO
GATES = 128
TRAIN = 64
HALF = 32
BINS = HALF + 2
SLOTS = PULSES + 2
GROUP = 6
ROWS = 144
PITCH = PULSES + 8
PIECES = ((0, 10), (10, 8), (18, 8), (26, 8))


def dft_matrix():
    freq = np.arange(PULSES)
    angle = (freq[:, None] * freq[None, :] % PULSES) * (2.0 * math.pi / PULSES)
    cosine = np.cos(angle) / math.sqrt(PULSES)
    sine = np.sin(angle) / math.sqrt(PULSES)
    return np.block([[cosine, sine], [-sine, cosine]]).astype(jnp.bfloat16)


def dot(a, b):
    return jnp.dot(a, b, preferred_element_type=F32)


def dot_nt(a, b):
    return lax.dot_general(a, b, (((1,), (1,)), ((), ())), preferred_element_type=F32)


def turned_by(x, shift):
    return pltpu.roll(x, shift % x.shape[0], 0) if shift else x


def kernel(
    sizes,
    off_hbm,
    cube_hbm,
    idx_hbm,
    guard_hbm,
    wts_hbm,
    dft_hbm,
    cov,
    matched_ref,
    pmap_ref,
    off_ref,
    cube,
    idx_ref,
    guard_ref,
    wts_ref,
    dft_ref,
    spec,
    bins_a,
    bins_b,
    train,
    train_halo,
    got_train,
    got_same,
    got_cross,
    send_wts,
    got_wts,
    lhs,
    filt_re,
    filt_im,
    send_part,
    got_part,
    send_quad,
    got_quad,
    sum_a,
    sum_b,
    ext_a,
    ext_b,
    rhs_re,
    rhs_im,
    lhs_cov,
    tiles,
    fetch_sem,
    send_sem,
    recv_sem,
    train_send,
    train_recv,
    same_send,
    same_recv,
    cross_send,
    cross_recv,
    a_send,
    a_recv,
    b_send,
    b_recv,
):
    n_z, n_xy, n_chan, n_rng = sizes
    n_a, n_b = n_xy * n_rng, n_z * 2
    chan, rng = lax.axis_index("chan"), lax.axis_index("rng")
    other = 1 - rng
    prev, following = lax.rem(chan + n_chan - 1, n_chan), lax.rem(chan + 1, n_chan)
    core = lax.rem(chan, 2)
    chip = chan // 2
    z, xy = chip // n_xy, lax.rem(chip, n_xy)
    my_a, my_b = xy * n_rng + rng, z * 2 + core

    def peer_a(step):
        slot = lax.rem(my_a + step, n_a)
        return slot, ((z * n_xy + slot // n_rng) * 2 + core, lax.rem(slot, n_rng))

    def peer_b(step):
        slot = lax.rem(my_b + step, n_b)
        return slot, (((slot // 2) * n_xy + xy) * 2 + lax.rem(slot, 2), rng)

    def remote(src, dst, send, recv, device):
        return pltpu.make_async_remote_copy(
            src_ref=src,
            dst_ref=dst,
            send_sem=send,
            recv_sem=recv,
            device_id=device,
            device_id_type=MESH,
        )

    fetches = [
        pltpu.make_async_copy(src, dst, fetch_sem.at[i])
        for i, (src, dst) in enumerate(
            (
                (off_hbm, off_ref),
                (wts_hbm, wts_ref),
                (idx_hbm, idx_ref),
                (guard_hbm, guard_ref),
                (dft_hbm, dft_ref),
                (cube_hbm, cube),
            )
        )
    ]
    for fetch in fetches:
        fetch.start()
    barrier = pltpu.get_barrier_semaphore()
    for device in ((prev, rng), (following, rng), (prev, other), (following, other)):
        pl.semaphore_signal(barrier, inc=1, device_id=device, device_id_type=MESH)

    def greet_a(step, carry):
        pl.semaphore_signal(barrier, inc=1, device_id=peer_a(step)[1], device_id_type=MESH)
        return carry

    def greet_b(step, carry):
        pl.semaphore_signal(barrier, inc=1, device_id=peer_b(step)[1], device_id_type=MESH)
        return carry

    lax.fori_loop(1, n_a, greet_a, 0)
    lax.fori_loop(1, n_b, greet_b, 0)

    fetches[0].wait()
    fetches[1].wait()
    lane = lax.broadcasted_iota(jnp.int32, (1, 128), 1)
    depth = lax.broadcasted_iota(jnp.int32, (96, 128), 0)
    placed = [[jnp.zeros((PULSES, 128), F32) for _ in range(3)] for _ in range(2)]
    for sub in range(2):
        for part in range(2):
            value = wts_ref[part, sub]
            for ahead in range(2):
                at = lax.rem(lane, 32) + (32 * ahead - 16 * sub) - off_ref[sub]
                fits = (at >= 0) & (at < SUB) & (lane // 32 == sub * 2 + part)
                for b in range(3):
                    hot = jnp.where(depth == jnp.where(fits, at + b * SUB, -1), 1.0, 0.0).astype(BF16)
                    placed[ahead][b] = placed[ahead][b] + dot(value, hot)
    for b in range(3):
        send_wts[b] = turned_by(placed[1][b], b - 1).astype(BF16)

    def fill_lhs(tables):
        for b in range(3):
            lhs[pl.ds(b * 2, PULSES, stride=8), :] = tables[b]
            lhs[pl.ds(b * 2 + 1, PULSES, stride=8), :] = pltpu.roll(tables[b], 64, 1)

    fetches[2].wait()
    fetches[3].wait()
    gate = lax.broadcasted_iota(jnp.int32, (GATES, 128), 0)
    wanted = jnp.concatenate([idx_ref[...], idx_ref[...]], axis=1)
    hits = jnp.where(gate == wanted, 1.0, 0.0)
    guard = jnp.broadcast_to(guard_ref[...].astype(F32), (8, GATES)).astype(BF16)
    keep = dot(guard, hits.astype(BF16))[0:1]
    pick = (hits * keep).astype(BF16)
    counts = dot_nt(jnp.full((8, 128), 0.5, BF16), pick)[0:1]

    pl.semaphore_wait(barrier, 4 + (n_a - 1) + (n_b - 1))
    wts_copy = remote(send_wts, got_wts, send_sem.at[0], recv_sem.at[0], (following, rng))
    wts_copy.start()

    fetches[4].wait()
    fetches[5].wait()
    table = dft_ref[...]

    def doppler(step, carry):
        for u in range(4):
            m = step * 8 + 2 * u
            pair = [jnp.concatenate([cube[0, m + v], cube[1, m + v]], axis=0) for v in range(2)]
            out = dot(table, jnp.concatenate(pair, axis=1))
            for v in range(2):
                for part in range(2):
                    start = pl.multiple_of((part * CH + m + v) * PITCH, 8)
                    spec[pl.ds(start, PULSES), :] = out[part * 64 : part * 64 + 64, v * 128 : v * 128 + 128]
        return carry

    lax.fori_loop(0, CH // 8, doppler, 0)

    left = lax.broadcasted_iota(jnp.int32, (CH, 128), 1) < TRAIN

    def gather_bins(step):
        for u in range(GROUP):
            k = lax.rem(step * GROUP + u + PULSES - 1, PULSES)
            re = spec[pl.ds(k, CH, stride=PITCH), :]
            im = spec[pl.ds(k + CH * PITCH, CH, stride=PITCH), :]
            bins_a[k] = jnp.concatenate([re, im], axis=0).astype(BF16)
            bins_b[k] = jnp.concatenate([im, -re], axis=0).astype(BF16)

    def choose_gates(step):
        rows = [bins_a[lax.rem(step * GROUP + u + PULSES - 1, PULSES)] for u in range(GROUP)]
        chosen = dot(jnp.concatenate(rows, axis=0), pick)
        halo = []
        for u in range(GROUP):
            tile = jnp.where(left, chosen[u * 64 : u * 64 + 32], chosen[u * 64 + 32 : u * 64 + 64])
            train[step * GROUP + u] = tile.astype(BF16)
            halo.append(tile[:HALO])
        start = pl.multiple_of(step * (GROUP * HALO), GROUP * HALO)
        train_halo[pl.ds(start, GROUP * HALO), :] = jnp.concatenate(halo, axis=0).astype(BF16)

    def per_bin(step, carry):
        choose_gates(step - 1)
        gather_bins(step)
        return carry

    gather_bins(0)
    lax.fori_loop(1, SLOTS // GROUP, per_bin, 0)
    choose_gates(SLOTS // GROUP - 1)

    def train_copy(piece):
        first, count = PIECES[piece]
        return remote(
            train.at[pl.ds(other * HALF + first, count)],
            got_train.at[pl.ds(first, count)],
            train_send.at[piece],
            train_recv.at[piece],
            (chan, other),
        )

    def same_copy(piece):
        first, count = PIECES[piece]
        start = pl.multiple_of(rng * (HALF * HALO) + first * HALO, 16)
        return remote(
            train_halo.at[pl.ds(start, count * HALO)],
            got_same.at[pl.ds(first * HALO, count * HALO)],
            same_send.at[piece],
            same_recv.at[piece],
            (prev, rng),
        )

    def cross_copy(piece):
        first, count = PIECES[piece]
        return remote(
            train.at[pl.ds(other * HALF + first, count)],
            got_cross.at[pl.ds(first, count)],
            cross_send.at[piece],
            cross_recv.at[piece],
            (prev, other),
        )

    def relay_copy(piece):
        first, count = PIECES[piece]
        return remote(
            got_train.at[pl.ds(first, count)],
            got_cross.at[pl.ds(first, count)],
            cross_send.at[piece],
            cross_recv.at[piece],
            (prev, rng),
        )

    train_copy(0).start()

    def filtered():
        def one(step, carry):
            for u in range(16):
                k = step * 16 + u
                row = pl.multiple_of(k * 8, 8)
                weight = lhs[pl.ds(row, 8), :][:, :64].astype(BF16)
                out = dot(weight, jnp.concatenate([bins_a[k], bins_b[k]], axis=1))
                filt_re[pl.ds(row, 8), :] = out[:, :128]
                filt_im[pl.ds(row, 8), :] = out[:, 128:]
            return carry

        lax.fori_loop(0, PULSES // 16, one, 0)
        sums = []
        for sub in range(2):
            for ref in (filt_re, filt_im):
                terms = [turned_by(ref[pl.ds(b * 2 + sub, PULSES, stride=8), :], 1 - b) for b in range(3)]
                sums.append(terms[0] + terms[1] + terms[2])
        return sums

    wts_copy.wait()
    fill_lhs([got_wts[b].astype(F32) for b in range(3)])
    for part, value in enumerate(filtered()):
        send_part[part] = value
    part_copy = remote(send_part, got_part, send_sem.at[1], recv_sem.at[1], (prev, rng))
    part_copy.start()
    for piece in range(len(PIECES)):
        if piece:
            train_copy(piece).start()
        same_copy(piece).start()

        @pl.when(core == 0)
        def _(piece=piece):
            cross_copy(piece).start()

    fill_lhs([turned_by(placed[0][b], b - 1) for b in range(3)])
    own = filtered()

    norms = []
    for sub in range(2):
        re, im = wts_ref[0, sub].astype(F32), wts_ref[1, sub].astype(F32)
        norms.append(jnp.sum(re * re + im * im, axis=1, keepdims=True))

    part_copy.wait()
    powers = []
    for sub in range(2):
        re = own[2 * sub] + got_part[2 * sub]
        im = own[2 * sub + 1] + got_part[2 * sub + 1]
        powers.append(re * re + im * im)
    sum_b[my_b] = jnp.sum(powers[0] + powers[1], axis=0, keepdims=True)

    def start_a(step, carry):
        device = peer_a(step)[1]
        remote(sum_a.at[my_a], sum_a.at[my_a], a_send.at[step], a_recv.at[my_a], device).start()
        return carry

    def start_b(step, carry):
        device = peer_b(step)[1]
        remote(sum_b.at[my_b], sum_b.at[my_b], b_send.at[step], b_recv.at[my_b], device).start()
        return carry

    def finish_a(step, carry):
        slot, device = peer_a(step)
        remote(sum_a.at[my_a], sum_a.at[slot], a_send.at[step], a_recv.at[slot], device).wait()
        return carry

    def finish_b(step, carry):
        slot, device = peer_b(step)
        remote(sum_b.at[my_b], sum_b.at[slot], b_send.at[step], b_recv.at[slot], device).wait()
        return carry

    lax.fori_loop(1, n_b, start_b, 0)
    quads = [jnp.sum(p * counts, axis=1, keepdims=True) for p in powers]
    send_quad[...] = jnp.where(lane < 64, quads[0], quads[1])
    quad_copy = remote(send_quad, got_quad, send_sem.at[2], recv_sem.at[2], (chan, other))
    quad_copy.start()

    low = lax.broadcasted_iota(jnp.int32, (SUB, 128), 1) < TRAIN

    def arrange(step, carry):
        rows = pl.multiple_of(step * (2 * HALO), 2 * HALO)
        same = got_same[pl.ds(rows, 2 * HALO), :].astype(F32)
        for u in range(2):
            k = step * 2 + u
            start = pl.multiple_of(k * EXT, 8)
            ext_a[pl.ds(start, CH), :] = train[rng * HALF + k].astype(F32)
            ext_a[pl.ds(start + CH, HALO), :] = same[u * HALO : u * HALO + HALO]
            ext_b[pl.ds(start, CH), :] = got_train[k].astype(F32)
            ext_b[pl.ds(start + CH, HALO), :] = got_cross[k].astype(F32)[:HALO]
        for u in range(2):
            k = step * 2 + u
            row = pl.multiple_of(k * SUB, SUB)
            for sub in range(2):
                start = k * EXT + 16 * sub + off_ref[sub]
                natural = [ext[pl.ds(start, SUB), :] for ext in (ext_a, ext_b)]
                turned = [pltpu.roll(x, 64, 1) for x in natural]
                rhs_re[sub, pl.ds(row, SUB), :] = jnp.concatenate(natural, axis=1).astype(BF16)
                rhs_im[sub, pl.ds(row, SUB), :] = jnp.concatenate([jnp.where(low, -x, x) for x in turned], axis=1).astype(
                    BF16
                )
                by_four = [
                    jnp.concatenate([ext[pl.ds(start + a, 8, stride=4), :] for a in range(4)], axis=0)
                    for ext in (ext_a, ext_b)
                ]
                lhs_cov[sub, pl.ds(row + 2 * SUB, SUB), :] = jnp.concatenate(by_four, axis=1).astype(BF16)
        return carry

    def tile(g, carry):
        row = pl.multiple_of(g * 128, 128)
        for sub in range(2):
            right = jnp.concatenate([rhs_re[sub, pl.ds(row, 128), :], rhs_im[sub, pl.ds(row, 128), :]], axis=0)
            tiles[sub, pl.ds(pl.multiple_of(g * 256, 256), 256), :] = dot_nt(lhs_cov[sub, pl.ds(row, 256), :], right)
        return carry

    col = lax.broadcasted_iota(jnp.int32, (8, 128), 1)

    def lay_out(g, carry):
        here = pl.multiple_of(g * 256, 256)
        for r in range(4):
            for sub in range(2):
                base = ((g * 4 + r) * 2 + sub) * ROWS
                for part in range(2):
                    lanes = slice(part * 128, part * 128 + 128)
                    by = [[], [], [], []]
                    for b in range(3):
                        block = tiles[sub, pl.ds(here + (r + b + 2) * 32, 32), lanes]
                        if r >= 2:
                            after = tiles[sub, pl.ds(here + 256 + (r + b - 2) * 32, 32), lanes]
                        for a in range(4):
                            x = block[a * 8 : a * 8 + 8]
                            if r >= 2:
                                x = jnp.where(col >= r * 32, x, after[a * 8 : a * 8 + 8])
                            shift = (3 * a - r) % 4 * 32
                            by[a].append((pltpu.roll(x, shift, 1) if shift else x) * (1.0 / 128.0))
                    for u, edge in enumerate((96, 64, 32)):
                        row = jnp.concatenate([jnp.where(col < edge, by[u][b], by[u + 1][b]) for b in range(3)], axis=0)
                        cov[pl.ds(base + 2 * u + part, 24, stride=6), :] = row
        return carry

    done_tiles = done_bins = 0
    for piece, (first, count) in enumerate(PIECES):
        train_copy(piece).wait()

        @pl.when(core == 1)
        def _(piece=piece):
            relay_copy(piece).start()

        same_copy(piece).wait()

        @pl.when(core == 1)
        def _(piece=piece):
            relay_copy(piece).wait()

        @pl.when(core == 0)
        def _(piece=piece):
            cross_copy(piece).wait()

        lax.fori_loop(first // 2, (first + count) // 2, arrange, 0)
        last = piece == len(PIECES) - 1
        ready = HALF // 4 + 1 if last else (first + count - 2) // 4
        lax.fori_loop(done_tiles, ready, tile, 0)
        lax.fori_loop(done_bins, ready - 1, lay_out, 0)
        done_tiles, done_bins = ready, ready - 1
        if piece == 1:
            lax.fori_loop(1, n_b, finish_b, 0)
            sum_a[my_a] = jnp.sum(sum_b[...], axis=0)
            lax.fori_loop(1, n_a, start_a, 0)

    quad_copy.wait()
    quad_sum = send_quad[...] + got_quad[...]
    for sub in range(2):
        quad = quad_sum[:, sub * 64 : sub * 64 + 1] * (1.0 / 128.0) + norms[sub]
        matched_ref[sub] = powers[sub] / quad

    lax.fori_loop(1, n_a, finish_a, 0)
    total = jnp.sum(jnp.sum(sum_a[...], axis=0), axis=1, keepdims=True)
    mean = total * (1.0 / (n_chan * n_rng * 2 * PULSES * GATES)) + 1e-6
    for sub in range(2):
        pmap_ref[sub] = powers[sub] / mean


def hand_out(cov, matched, pmap, cov_out, matched_out, pmap_out, sem):
    pairs = ((cov, cov_out), (matched, matched_out), (pmap, pmap_out))
    copies = [pltpu.make_async_copy(src, dst, sem.at[i]) for i, (src, dst) in enumerate(pairs)]
    for copy in copies:
        copy.start()
    for copy in copies:
        copy.wait()


def local(sizes, radar_cube, offsets, train_index, guard_mask, weights):
    n_z, n_xy, n_chan, n_rng = sizes
    n_a, n_b = n_xy * n_rng, n_z * 2
    n_pieces = len(PIECES)
    dma = pltpu.SemaphoreType.DMA
    vmem = pl.BlockSpec(memory_space=pltpu.VMEM)
    hbm = pl.BlockSpec(memory_space=pltpu.HBM)
    rows = HALF * 2 * ROWS
    shapes = (
        jax.ShapeDtypeStruct((rows, 128), F32),
        jax.ShapeDtypeStruct((2, PULSES, GATES), F32),
        jax.ShapeDtypeStruct((2, PULSES, GATES), F32),
    )
    held = pl.pallas_call(
        functools.partial(kernel, sizes),
        out_shape=shapes,
        in_specs=[hbm] * 6,
        out_specs=(vmem, vmem, vmem),
        scratch_shapes=[
            pltpu.SMEM((2,), jnp.int32),
            pltpu.VMEM((2, CH, PULSES, GATES), BF16),
            pltpu.VMEM((1, TRAIN), jnp.int32),
            pltpu.VMEM((1, GATES), jnp.int32),
            pltpu.VMEM((2, 2, PULSES, 96), BF16),
            pltpu.VMEM((128, 128), BF16),
            pltpu.VMEM((2 * CH * PITCH, GATES), F32),
            pltpu.VMEM((PULSES, 2 * CH, GATES), BF16),
            pltpu.VMEM((PULSES, 2 * CH, GATES), BF16),
            pltpu.VMEM((SLOTS, CH, 128), BF16),
            pltpu.VMEM((SLOTS * HALO, 128), BF16),
            pltpu.VMEM((BINS, CH, 128), BF16),
            pltpu.VMEM((BINS * HALO, 128), BF16),
            pltpu.VMEM((BINS, CH, 128), BF16),
            pltpu.VMEM((3, PULSES, 128), BF16),
            pltpu.VMEM((3, PULSES, 128), BF16),
            pltpu.VMEM((PULSES * 8, 128), F32),
            pltpu.VMEM((PULSES * 8, 128), F32),
            pltpu.VMEM((PULSES * 8, 128), F32),
            pltpu.VMEM((4, PULSES, GATES), F32),
            pltpu.VMEM((4, PULSES, GATES), F32),
            pltpu.VMEM((PULSES, 128), F32),
            pltpu.VMEM((PULSES, 128), F32),
            pltpu.VMEM((n_a, 1, 128), F32),
            pltpu.VMEM((n_b, 1, 128), F32),
            pltpu.VMEM((BINS * EXT, 128), F32),
            pltpu.VMEM((BINS * EXT, 128), F32),
            pltpu.VMEM((2, (BINS + 2) * SUB, 256), BF16),
            pltpu.VMEM((2, (BINS + 2) * SUB, 256), BF16),
            pltpu.VMEM((2, (BINS + 6) * SUB, 256), BF16),
            pltpu.VMEM((2, (HALF // 4 + 1) * 256, 256), F32),
            dma((6,)),
            dma((3,)),
            dma((3,)),
            dma((n_pieces,)),
            dma((n_pieces,)),
            dma((n_pieces,)),
            dma((n_pieces,)),
            dma((n_pieces,)),
            dma((n_pieces,)),
            dma((n_a,)),
            dma((n_a,)),
            dma((n_b,)),
            dma((n_b,)),
        ],
        compiler_params=pltpu.CompilerParams(
            collective_id=0, has_side_effects=True, vmem_limit_bytes=32 * 1024 * 1024
        ),
    )(
        *(
            pltpu.with_memory_space_constraint(x, pltpu.HBM)
            for x in (
                offsets,
                radar_cube,
                train_index.reshape(1, -1),
                guard_mask.reshape(1, -1),
                weights,
                jnp.asarray(dft_matrix()),
            )
        )
    )
    cov, matched, pmap = pl.pallas_call(
        hand_out,
        out_shape=shapes,
        in_specs=[vmem] * 3,
        out_specs=(hbm, hbm, hbm),
        scratch_shapes=[dma((3,))],
        compiler_params=pltpu.CompilerParams(vmem_limit_bytes=1024 * 1024),
    )(*held)
    cov = cov.reshape(HALF, 2, ROWS // 2, 2, 128).transpose(0, 1, 3, 2, 4).reshape(HALF, 2, 2, ROWS * 64)
    return cov, matched, pmap


def solution(mesh):
    n_chan, n_rng = mesh.shape["chan"], mesh.shape["rng"]
    n_xy = 8 if n_chan >= 64 else 2
    sizes = (n_chan // (2 * n_xy), n_xy, n_chan, n_rng)
    return jax.shard_map(
        functools.partial(local, sizes),
        mesh=mesh,
        in_specs=(
            P(None, "chan", None, "rng"),
            P("chan"),
            P("rng"),
            P("rng"),
            P(None, "chan", None, None),
        ),
        out_specs=(P("rng", "chan", None, None), P("chan", None, "rng"), P("chan", None, "rng")),
        check_vma=False,
    )
```

time: 54.2 us -> 37 us (0.68)
  Pallas kernels: 47.3 us -> 36.3 us
  local copies, waits for them, and re-layouts: 6.14 us -> 0 us
    pallas_call x1 -> x2, Pallas kernels: 47.3 us -> 36.3 us  [the longest x1 34 us: local(): pl.pallas_call(functools.partial(kernel, sizes), out_shape=shapes, in_spe...]
    unnamed x7 -> x0, local copies, waits for them, and re-layouts: 6.14 us -> none
where the time goes in v1:
time: 37 us; the launch traced here: 36.9 us
  Pallas kernels  36.3 us (98%)
  between operations  0.64 us (2%)
    pallas_call x1, Pallas kernels, local(): pl.pallas_call(functools.partial(kernel, sizes), out_shape=shapes, in_spe...  34 us
    pallas_call x1, Pallas kernels, local(): pl.pallas_call(hand_out, out_shape=shapes, in_specs=[vmem] * 3, out_specs...  2.23 us

profile of v1, /device:TPU:1, one launch (start us, length us, event | category | flops | bytes accessed | tf_op | source)
XLA Modules:
  0.0 36.9 jit_solution(5497705317153793639)
XLA Ops:
  0.6 34.0 %shard_map.85 = (f32[9216,128]{1,0:T(8,128)S(1)}, f32[2,64,128]{2,1,0:T(8,128)S(1)}, f32[2,64,128]{2,1,0:T(8,128)S(1)}) custom-call(s32[2]{0:T(128)} %off_hbm.1, bf16[2,32,64,128]{3,2,1,0:T(8,128)(2,1)} %cube_hbm.1, s32[1,64]{1,0:T(1,128)} %bitcast.7, s32[1,128]{1,0:T(1,128)} %bitcast.8, bf16[2,2,64,96]{3,2,1,0:T(8,128)(2,1)} %wts_hbm.1, ...), custom_call_target="tpu_custom_call" | custom-call | tf_op jit(solution)/shard_map/pallas_call | solution.py:494
  34.7 2.2 %shard_map.86 = (f32[9216,128]{1,0:T(8,128)}, f32[2,64,128]{2,1,0:T(8,128)}, f32[2,64,128]{2,1,0:T(8,128)}) custom-call(f32[9216,128]{1,0:T(8,128)S(1)} %get-tuple-element.9.cov, f32[2,64,128]{2,1,0:T(8,128)S(1)} %get-tuple-element.10.matched, f32[2,64,128]{2,1,0:T(8,128)S(1)} %get-tuple-element.11.pmap), custom_call_target="tpu_custom_call" | custom-call | tf_op jit(solution)/shard_map/pallas_call | solution.py:561

commit v2 on v1

--- a/solution.py
+++ b/solution.py
@@ -23,8 +23,9 @@
 HALF = 32
 BINS = HALF + 2
 SLOTS = PULSES + 2
-GROUP = 6
+GROUP = 22
 ROWS = 144
+PARTS = 4
 PITCH = PULSES + 8
 PIECES = ((0, 10), (10, 8), (18, 8), (26, 8))
 
@@ -67,8 +68,7 @@
     wts_ref,
     dft_ref,
     spec,
-    bins_a,
-    bins_b,
+    bins,
     train,
     train_halo,
     got_train,
@@ -76,7 +76,8 @@
     got_cross,
     send_wts,
     got_wts,
-    lhs,
+    lhs_re,
+    lhs_im,
     filt_re,
     filt_im,
     send_part,
@@ -94,16 +95,9 @@
     fetch_sem,
     send_sem,
     recv_sem,
-    train_send,
     train_recv,
-    same_send,
     same_recv,
-    cross_send,
     cross_recv,
-    a_send,
-    a_recv,
-    b_send,
-    b_recv,
 ):
     n_z, n_xy, n_chan, n_rng = sizes
     n_a, n_b = n_xy * n_rng, n_z * 2
@@ -117,11 +111,11 @@
 
     def peer_a(step):
         slot = lax.rem(my_a + step, n_a)
-        return slot, ((z * n_xy + slot // n_rng) * 2 + core, lax.rem(slot, n_rng))
+        return (z * n_xy + slot // n_rng) * 2 + core, lax.rem(slot, n_rng)
 
     def peer_b(step):
         slot = lax.rem(my_b + step, n_b)
-        return slot, (((slot // 2) * n_xy + xy) * 2 + lax.rem(slot, 2), rng)
+        return ((slot // 2) * n_xy + xy) * 2 + lax.rem(slot, 2), rng
 
     def remote(src, dst, send, recv, device):
         return pltpu.make_async_remote_copy(
@@ -152,16 +146,10 @@
     for device in ((prev, rng), (following, rng), (prev, other), (following, other)):
         pl.semaphore_signal(barrier, inc=1, device_id=device, device_id_type=MESH)
 
-    def greet_a(step, carry):
-        pl.semaphore_signal(barrier, inc=1, device_id=peer_a(step)[1], device_id_type=MESH)
-        return carry
-
-    def greet_b(step, carry):
-        pl.semaphore_signal(barrier, inc=1, device_id=peer_b(step)[1], device_id_type=MESH)
-        return carry
-
-    lax.fori_loop(1, n_a, greet_a, 0)
-    lax.fori_loop(1, n_b, greet_b, 0)
+    for step in range(1, n_b):
+        pl.semaphore_signal(barrier, inc=1, device_id=peer_b(step), device_id_type=MESH)
+    for step in range(1, n_a):
+        pl.semaphore_signal(barrier, inc=1, device_id=peer_a(step), device_id_type=MESH)
 
     fetches[0].wait()
     fetches[1].wait()
@@ -180,10 +168,16 @@
     for b in range(3):
         send_wts[b] = turned_by(placed[1][b], b - 1).astype(BF16)
 
+    first_half = lax.rem(lax.broadcasted_iota(jnp.int32, (PULSES, 128), 1), 64) < 32
+
     def fill_lhs(tables):
         for b in range(3):
-            lhs[pl.ds(b * 2, PULSES, stride=8), :] = tables[b]
-            lhs[pl.ds(b * 2 + 1, PULSES, stride=8), :] = pltpu.roll(tables[b], 64, 1)
+            x = tables[b]
+            up, down = pltpu.roll(x, 96, 1), pltpu.roll(x, 32, 1)
+            lhs_re[pl.ds(b * 2, PULSES, stride=8), :] = x
+            lhs_re[pl.ds(b * 2 + 1, PULSES, stride=8), :] = pltpu.roll(x, 64, 1)
+            lhs_im[pl.ds(b * 2, PULSES, stride=8), :] = jnp.where(first_half, -up, down)
+            lhs_im[pl.ds(b * 2 + 1, PULSES, stride=8), :] = jnp.where(first_half, -down, up)
 
     fetches[2].wait()
     fetches[3].wait()
@@ -194,10 +188,6 @@
     keep = dot(guard, hits.astype(BF16))[0:1]
     pick = (hits * keep).astype(BF16)
     counts = dot_nt(jnp.full((8, 128), 0.5, BF16), pick)[0:1]
-
-    pl.semaphore_wait(barrier, 4 + (n_a - 1) + (n_b - 1))
-    wts_copy = remote(send_wts, got_wts, send_sem.at[0], recv_sem.at[0], (following, rng))
-    wts_copy.start()
 
     fetches[4].wait()
     fetches[5].wait()
@@ -216,6 +206,10 @@
 
     lax.fori_loop(0, CH // 8, doppler, 0)
 
+    pl.semaphore_wait(barrier, 4 + (n_a - 1) + (n_b - 1))
+    wts_copy = remote(send_wts, got_wts, send_sem.at[0], recv_sem.at[0], (following, rng))
+    wts_copy.start()
+
     left = lax.broadcasted_iota(jnp.int32, (CH, 128), 1) < TRAIN
 
     def gather_bins(step):
@@ -223,11 +217,10 @@
             k = lax.rem(step * GROUP + u + PULSES - 1, PULSES)
             re = spec[pl.ds(k, CH, stride=PITCH), :]
             im = spec[pl.ds(k + CH * PITCH, CH, stride=PITCH), :]
-            bins_a[k] = jnp.concatenate([re, im], axis=0).astype(BF16)
-            bins_b[k] = jnp.concatenate([im, -re], axis=0).astype(BF16)
+            bins[k] = jnp.concatenate([re, im], axis=0).astype(BF16)
 
     def choose_gates(step):
-        rows = [bins_a[lax.rem(step * GROUP + u + PULSES - 1, PULSES)] for u in range(GROUP)]
+        rows = [bins[lax.rem(step * GROUP + u + PULSES - 1, PULSES)] for u in range(GROUP)]
         chosen = dot(jnp.concatenate(rows, axis=0), pick)
         halo = []
         for u in range(GROUP):
@@ -251,7 +244,7 @@
         return remote(
             train.at[pl.ds(other * HALF + first, count)],
             got_train.at[pl.ds(first, count)],
-            train_send.at[piece],
+            send_sem.at[3],
             train_recv.at[piece],
             (chan, other),
         )
@@ -262,7 +255,7 @@
         return remote(
             train_halo.at[pl.ds(start, count * HALO)],
             got_same.at[pl.ds(first * HALO, count * HALO)],
-            same_send.at[piece],
+            send_sem.at[4],
             same_recv.at[piece],
             (prev, rng),
         )
@@ -272,7 +265,7 @@
         return remote(
             train.at[pl.ds(other * HALF + first, count)],
             got_cross.at[pl.ds(first, count)],
-            cross_send.at[piece],
+            send_sem.at[5],
             cross_recv.at[piece],
             (prev, other),
         )
@@ -282,25 +275,38 @@
         return remote(
             got_train.at[pl.ds(first, count)],
             got_cross.at[pl.ds(first, count)],
-            cross_send.at[piece],
+            send_sem.at[5],
             cross_recv.at[piece],
             (prev, rng),
         )
 
-    train_copy(0).start()
+    def send_piece(piece):
+        train_copy(piece).start()
+
+        @pl.when(core == 0)
+        def _():
+            same_copy(piece).start()
+            cross_copy(piece).start()
+
+    send_piece(0)
+
+    @pl.when(core == 1)
+    def _():
+        for piece in range(len(PIECES)):
+            same_copy(piece).start()
 
     def filtered():
         def one(step, carry):
-            for u in range(16):
-                k = step * 16 + u
+            for u in range(32):
+                k = step * 32 + u
                 row = pl.multiple_of(k * 8, 8)
-                weight = lhs[pl.ds(row, 8), :][:, :64].astype(BF16)
-                out = dot(weight, jnp.concatenate([bins_a[k], bins_b[k]], axis=1))
-                filt_re[pl.ds(row, 8), :] = out[:, :128]
-                filt_im[pl.ds(row, 8), :] = out[:, 128:]
+                weight = jnp.concatenate([lhs_re[pl.ds(row, 8), :], lhs_im[pl.ds(row, 8), :]], axis=0)
+                out = dot(weight[:, :64].astype(BF16), bins[k])
+                filt_re[pl.ds(row, 8), :] = out[:8]
+                filt_im[pl.ds(row, 8), :] = out[8:]
             return carry
 
-        lax.fori_loop(0, PULSES // 16, one, 0)
+        lax.fori_loop(0, PULSES // 32, one, 0)
         sums = []
         for sub in range(2):
             for ref in (filt_re, filt_im):
@@ -314,14 +320,6 @@
         send_part[part] = value
     part_copy = remote(send_part, got_part, send_sem.at[1], recv_sem.at[1], (prev, rng))
     part_copy.start()
-    for piece in range(len(PIECES)):
-        if piece:
-            train_copy(piece).start()
-        same_copy(piece).start()
-
-        @pl.when(core == 0)
-        def _(piece=piece):
-            cross_copy(piece).start()
 
     fill_lhs([turned_by(placed[0][b], b - 1) for b in range(3)])
     own = filtered()
@@ -331,39 +329,13 @@
         re, im = wts_ref[0, sub].astype(F32), wts_ref[1, sub].astype(F32)
         norms.append(jnp.sum(re * re + im * im, axis=1, keepdims=True))
 
-    part_copy.wait()
-    powers = []
-    for sub in range(2):
-        re = own[2 * sub] + got_part[2 * sub]
-        im = own[2 * sub + 1] + got_part[2 * sub + 1]
-        powers.append(re * re + im * im)
-    sum_b[my_b] = jnp.sum(powers[0] + powers[1], axis=0, keepdims=True)
-
-    def start_a(step, carry):
-        device = peer_a(step)[1]
-        remote(sum_a.at[my_a], sum_a.at[my_a], a_send.at[step], a_recv.at[my_a], device).start()
-        return carry
-
-    def start_b(step, carry):
-        device = peer_b(step)[1]
-        remote(sum_b.at[my_b], sum_b.at[my_b], b_send.at[step], b_recv.at[my_b], device).start()
-        return carry
-
-    def finish_a(step, carry):
-        slot, device = peer_a(step)
-        remote(sum_a.at[my_a], sum_a.at[slot], a_send.at[step], a_recv.at[slot], device).wait()
-        return carry
-
-    def finish_b(step, carry):
-        slot, device = peer_b(step)
-        remote(sum_b.at[my_b], sum_b.at[slot], b_send.at[step], b_recv.at[slot], device).wait()
-        return carry
-
-    lax.fori_loop(1, n_b, start_b, 0)
-    quads = [jnp.sum(p * counts, axis=1, keepdims=True) for p in powers]
-    send_quad[...] = jnp.where(lane < 64, quads[0], quads[1])
-    quad_copy = remote(send_quad, got_quad, send_sem.at[2], recv_sem.at[2], (chan, other))
-    quad_copy.start()
+    def spread(ref, peers, sem, peer):
+        for step in range(1, peers):
+            remote(ref.at[peers - 1], ref.at[step - 1], send_sem.at[sem], recv_sem.at[sem - 3], peer(step)).start()
+
+    def collect(ref, peers, sem, peer):
+        span = ref.at[pl.ds(0, peers - 1)]
+        remote(span, span, send_sem.at[sem], recv_sem.at[sem - 3], peer(1)).wait()
 
     low = lax.broadcasted_iota(jnp.int32, (SUB, 128), 1) < TRAIN
 
@@ -395,12 +367,11 @@
                 lhs_cov[sub, pl.ds(row + 2 * SUB, SUB), :] = jnp.concatenate(by_four, axis=1).astype(BF16)
         return carry
 
-    def tile(g, carry):
-        row = pl.multiple_of(g * 128, 128)
+    def tile(g):
+        row = g * 128
         for sub in range(2):
             right = jnp.concatenate([rhs_re[sub, pl.ds(row, 128), :], rhs_im[sub, pl.ds(row, 128), :]], axis=0)
-            tiles[sub, pl.ds(pl.multiple_of(g * 256, 256), 256), :] = dot_nt(lhs_cov[sub, pl.ds(row, 256), :], right)
-        return carry
+            tiles[sub, pl.ds(g * 256, 256), :] = dot_nt(lhs_cov[sub, pl.ds(row, 256), :], right)
 
     col = lax.broadcasted_iota(jnp.int32, (8, 128), 1)
 
@@ -427,34 +398,55 @@
                         cov[pl.ds(base + 2 * u + part, 24, stride=6), :] = row
         return carry
 
-    done_tiles = done_bins = 0
-    for piece, (first, count) in enumerate(PIECES):
-        train_copy(piece).wait()
+    def pass_on(piece):
+        train_copy(piece).wait_recv()
 
         @pl.when(core == 1)
-        def _(piece=piece):
+        def _():
             relay_copy(piece).start()
 
-        same_copy(piece).wait()
-
-        @pl.when(core == 1)
-        def _(piece=piece):
-            relay_copy(piece).wait()
-
-        @pl.when(core == 0)
-        def _(piece=piece):
-            cross_copy(piece).wait()
-
+    ready = [(first + count - 2) // 4 for first, count in PIECES]
+    ready[-1] = HALF // 4 + 1
+
+    def cover(piece):
+        first, count = PIECES[piece]
+        same_copy(piece).wait_recv()
+        relay_copy(piece).wait_recv()
         lax.fori_loop(first // 2, (first + count) // 2, arrange, 0)
-        last = piece == len(PIECES) - 1
-        ready = HALF // 4 + 1 if last else (first + count - 2) // 4
-        lax.fori_loop(done_tiles, ready, tile, 0)
-        lax.fori_loop(done_bins, ready - 1, lay_out, 0)
-        done_tiles, done_bins = ready, ready - 1
-        if piece == 1:
-            lax.fori_loop(1, n_b, finish_b, 0)
-            sum_a[my_a] = jnp.sum(sum_b[...], axis=0)
-            lax.fori_loop(1, n_a, start_a, 0)
+        begin = ready[piece - 1] if piece else 0
+        for g in range(begin, ready[piece]):
+            tile(g)
+        lax.fori_loop(max(begin - 1, 0), ready[piece] - 1, lay_out, 0)
+
+    pass_on(0)
+    cover(0)
+    part_copy.wait()
+    powers = []
+    for sub in range(2):
+        re = own[2 * sub] + got_part[2 * sub]
+        im = own[2 * sub + 1] + got_part[2 * sub + 1]
+        powers.append(re * re + im * im)
+    sum_a[n_a - 1] = jnp.sum(powers[0] + powers[1], axis=0, keepdims=True)
+
+    spread(sum_a, n_a, 7, peer_a)
+    for piece in range(1, len(PIECES)):
+        send_piece(piece)
+    quads = [jnp.sum(p * counts, axis=1, keepdims=True) for p in powers]
+    send_quad[...] = jnp.where(lane < 64, quads[0], quads[1])
+    quad_copy = remote(send_quad, got_quad, send_sem.at[2], recv_sem.at[2], (chan, other))
+    quad_copy.start()
+
+
+    pass_on(1)
+    cover(1)
+
+    collect(sum_a, n_a, 7, peer_a)
+    sum_b[n_b - 1] = jnp.sum(sum_a[...], axis=0)
+    spread(sum_b, n_b, 6, peer_b)
+    pass_on(2)
+    cover(2)
+    pass_on(3)
+    cover(3)
 
     quad_copy.wait()
     quad_sum = send_quad[...] + got_quad[...]
@@ -462,15 +454,21 @@
         quad = quad_sum[:, sub * 64 : sub * 64 + 1] * (1.0 / 128.0) + norms[sub]
         matched_ref[sub] = powers[sub] / quad
 
-    lax.fori_loop(1, n_a, finish_a, 0)
-    total = jnp.sum(jnp.sum(sum_a[...], axis=0), axis=1, keepdims=True)
+    collect(sum_b, n_b, 6, peer_b)
+    total = jnp.sum(jnp.sum(sum_b[...], axis=0), axis=1, keepdims=True)
     mean = total * (1.0 / (n_chan * n_rng * 2 * PULSES * GATES)) + 1e-6
     for sub in range(2):
         pmap_ref[sub] = powers[sub] / mean
+    train_span, halo_span = train.at[pl.ds(0, BINS)], train_halo.at[pl.ds(0, BINS * HALO)]
+    remote(train_span, got_train, send_sem.at[3], train_recv.at[0], (chan, other)).wait_send()
+    remote(halo_span, got_same, send_sem.at[4], same_recv.at[0], (prev, rng)).wait_send()
+    remote(train_span, got_cross, send_sem.at[5], cross_recv.at[0], (prev, rng)).wait_send()
 
 
 def hand_out(cov, matched, pmap, cov_out, matched_out, pmap_out, sem):
-    pairs = ((cov, cov_out), (matched, matched_out), (pmap, pmap_out))
+    rows = cov.shape[0] // PARTS
+    parts = [(cov.at[pl.ds(i * rows, rows)], cov_out.at[pl.ds(i * rows, rows)]) for i in range(PARTS)]
+    pairs = (*parts, (matched, matched_out), (pmap, pmap_out))
     copies = [pltpu.make_async_copy(src, dst, sem.at[i]) for i, (src, dst) in enumerate(pairs)]
     for copy in copies:
         copy.start()
@@ -505,7 +503,6 @@
             pltpu.VMEM((128, 128), BF16),
             pltpu.VMEM((2 * CH * PITCH, GATES), F32),
             pltpu.VMEM((PULSES, 2 * CH, GATES), BF16),
-            pltpu.VMEM((PULSES, 2 * CH, GATES), BF16),
             pltpu.VMEM((SLOTS, CH, 128), BF16),
             pltpu.VMEM((SLOTS * HALO, 128), BF16),
             pltpu.VMEM((BINS, CH, 128), BF16),
@@ -513,6 +510,7 @@
             pltpu.VMEM((BINS, CH, 128), BF16),
             pltpu.VMEM((3, PULSES, 128), BF16),
             pltpu.VMEM((3, PULSES, 128), BF16),
+            pltpu.VMEM((PULSES * 8, 128), F32),
             pltpu.VMEM((PULSES * 8, 128), F32),
             pltpu.VMEM((PULSES * 8, 128), F32),
             pltpu.VMEM((PULSES * 8, 128), F32),
@@ -529,18 +527,11 @@
             pltpu.VMEM((2, (BINS + 6) * SUB, 256), BF16),
             pltpu.VMEM((2, (HALF // 4 + 1) * 256, 256), F32),
             dma((6,)),
-            dma((3,)),
-            dma((3,)),
+            dma((8,)),
+            dma((5,)),
             dma((n_pieces,)),
             dma((n_pieces,)),
             dma((n_pieces,)),
-            dma((n_pieces,)),
-            dma((n_pieces,)),
-            dma((n_pieces,)),
-            dma((n_a,)),
-            dma((n_a,)),
-            dma((n_b,)),
-            dma((n_b,)),
         ],
         compiler_params=pltpu.CompilerParams(
             collective_id=0, has_side_effects=True, vmem_limit_bytes=32 * 1024 * 1024
@@ -563,7 +554,7 @@
         out_shape=shapes,
         in_specs=[vmem] * 3,
         out_specs=(hbm, hbm, hbm),
-        scratch_shapes=[dma((3,))],
+        scratch_shapes=[dma((PARTS + 2,))],
         compiler_params=pltpu.CompilerParams(vmem_limit_bytes=1024 * 1024),
     )(*held)
     cov = cov.reshape(HALF, 2, ROWS // 2, 2, 128).transpose(0, 1, 3, 2, 4).reshape(HALF, 2, 2, ROWS * 64)

time: 37 us -> 33.6 us (0.908)
  Pallas kernels: 36.3 us -> 32.9 us
    pallas_call x1, Pallas kernels: 34 us -> 30.6 us  [local(): pl.pallas_call(functools.partial(kernel, sizes), out_shape=shapes, in_spe...]
where the time goes in v2:
time: 33.6 us; the launch traced here: 33.5 us
  Pallas kernels  32.9 us (98%)
  between operations  0.64 us (2%)
    pallas_call x1, Pallas kernels, local(): pl.pallas_call(functools.partial(kernel, sizes), out_shape=shapes, in_spe...  30.6 us
    pallas_call x1, Pallas kernels, local(): pl.pallas_call(hand_out, out_shape=shapes, in_specs=[vmem] * 3, out_specs...  2.26 us

profile of v2, /device:TPU:1, one launch (start us, length us, event | category | flops | bytes accessed | tf_op | source)
XLA Modules:
  0.0 33.5 jit_solution(11446923655790461239)
XLA Ops:
  0.6 30.6 %shard_map.85 = (f32[9216,128]{1,0:T(8,128)S(1)}, f32[2,64,128]{2,1,0:T(8,128)S(1)}, f32[2,64,128]{2,1,0:T(8,128)S(1)}) custom-call(s32[2]{0:T(128)} %off_hbm.1, bf16[2,32,64,128]{3,2,1,0:T(8,128)(2,1)} %cube_hbm.1, s32[1,64]{1,0:T(1,128)} %bitcast.7, s32[1,128]{1,0:T(1,128)} %bitcast.8, bf16[2,2,64,96]{3,2,1,0:T(8,128)(2,1)} %wts_hbm.1, ...), custom_call_target="tpu_custom_call" | custom-call | tf_op jit(solution)/shard_map/pallas_call | solution.py:492
  31.3 2.3 %shard_map.86 = (f32[9216,128]{1,0:T(8,128)}, f32[2,64,128]{2,1,0:T(8,128)}, f32[2,64,128]{2,1,0:T(8,128)}) custom-call(f32[9216,128]{1,0:T(8,128)S(1)} %get-tuple-element.9.cov, f32[2,64,128]{2,1,0:T(8,128)S(1)} %get-tuple-element.10.matched, f32[2,64,128]{2,1,0:T(8,128)S(1)} %get-tuple-element.11.pmap), custom_call_target="tpu_custom_call" | custom-call | tf_op jit(solution)/shard_map/pallas_call | solution.py:552

commit v3 on v2

--- a/solution.py
+++ b/solution.py
@@ -24,8 +24,8 @@
 BINS = HALF + 2
 SLOTS = PULSES + 2
 GROUP = 22
+HEAD = 3
 ROWS = 144
-PARTS = 4
 PITCH = PULSES + 8
 PIECES = ((0, 10), (10, 8), (18, 8), (26, 8))
 
@@ -48,6 +48,31 @@
 
 def turned_by(x, shift):
     return pltpu.roll(x, shift % x.shape[0], 0) if shift else x
+
+
+def lay_out(tiles, cov, origin, g, carry):
+    col = lax.broadcasted_iota(jnp.int32, (8, 128), 1)
+    here = pl.multiple_of(g * 256, 256)
+    for r in range(4):
+        for sub in range(2):
+            base = (((g - origin) * 4 + r) * 2 + sub) * ROWS
+            for part in range(2):
+                lanes = slice(part * 128, part * 128 + 128)
+                by = [[], [], [], []]
+                for b in range(3):
+                    block = tiles[sub, pl.ds(here + (r + b + 2) * 32, 32), lanes]
+                    if r >= 2:
+                        after = tiles[sub, pl.ds(here + 256 + (r + b - 2) * 32, 32), lanes]
+                    for a in range(4):
+                        x = block[a * 8 : a * 8 + 8]
+                        if r >= 2:
+                            x = jnp.where(col >= r * 32, x, after[a * 8 : a * 8 + 8])
+                        shift = (3 * a - r) % 4 * 32
+                        by[a].append(pltpu.roll(x, shift, 1) if shift else x)
+                for u, edge in enumerate((96, 64, 32)):
+                    row = jnp.concatenate([jnp.where(col < edge, by[u][b], by[u + 1][b]) for b in range(3)], axis=0)
+                    cov[pl.ds(base + 2 * u + part, 24, stride=6), :] = row
+    return carry
 
 
 def kernel(
@@ -58,7 +83,8 @@
     guard_hbm,
     wts_hbm,
     dft_hbm,
-    cov,
+    tiles,
+    head,
     matched_ref,
     pmap_ref,
     off_ref,
@@ -91,7 +117,6 @@
     rhs_re,
     rhs_im,
     lhs_cov,
-    tiles,
     fetch_sem,
     send_sem,
     recv_sem,
@@ -140,8 +165,8 @@
             )
         )
     ]
-    for fetch in fetches:
-        fetch.start()
+    for i in (1, 0, 5, 4):
+        fetches[i].start()
     barrier = pltpu.get_barrier_semaphore()
     for device in ((prev, rng), (following, rng), (prev, other), (following, other)):
         pl.semaphore_signal(barrier, inc=1, device_id=device, device_id_type=MESH)
@@ -150,44 +175,41 @@
         pl.semaphore_signal(barrier, inc=1, device_id=peer_b(step), device_id_type=MESH)
     for step in range(1, n_a):
         pl.semaphore_signal(barrier, inc=1, device_id=peer_a(step), device_id_type=MESH)
+    for fetch in fetches[2:4]:
+        fetch.start()
 
     fetches[0].wait()
     fetches[1].wait()
     lane = lax.broadcasted_iota(jnp.int32, (1, 128), 1)
     depth = lax.broadcasted_iota(jnp.int32, (96, 128), 0)
     placed = [[jnp.zeros((PULSES, 128), F32) for _ in range(3)] for _ in range(2)]
+    group, place = lane // 32, lax.rem(lane, 32)
     for sub in range(2):
         for part in range(2):
             value = wts_ref[part, sub]
             for ahead in range(2):
-                at = lax.rem(lane, 32) + (32 * ahead - 16 * sub) - off_ref[sub]
-                fits = (at >= 0) & (at < SUB) & (lane // 32 == sub * 2 + part)
+                if ahead:
+                    channel = CH + (place if sub else place - HALO)
+                    mine = (group == part) & ((place < HALO) if sub else (place >= HALO))
+                else:
+                    channel = place
+                    mine = group == sub * 2 + part
+                at = channel - 16 * sub - off_ref[sub]
+                fits = (at >= 0) & (at < SUB) & mine
                 for b in range(3):
                     hot = jnp.where(depth == jnp.where(fits, at + b * SUB, -1), 1.0, 0.0).astype(BF16)
                     placed[ahead][b] = placed[ahead][b] + dot(value, hot)
     for b in range(3):
-        send_wts[b] = turned_by(placed[1][b], b - 1).astype(BF16)
-
-    first_half = lax.rem(lax.broadcasted_iota(jnp.int32, (PULSES, 128), 1), 64) < 32
-
-    def fill_lhs(tables):
-        for b in range(3):
-            x = tables[b]
-            up, down = pltpu.roll(x, 96, 1), pltpu.roll(x, 32, 1)
-            lhs_re[pl.ds(b * 2, PULSES, stride=8), :] = x
-            lhs_re[pl.ds(b * 2 + 1, PULSES, stride=8), :] = pltpu.roll(x, 64, 1)
-            lhs_im[pl.ds(b * 2, PULSES, stride=8), :] = jnp.where(first_half, -up, down)
-            lhs_im[pl.ds(b * 2 + 1, PULSES, stride=8), :] = jnp.where(first_half, -down, up)
-
-    fetches[2].wait()
-    fetches[3].wait()
-    gate = lax.broadcasted_iota(jnp.int32, (GATES, 128), 0)
-    wanted = jnp.concatenate([idx_ref[...], idx_ref[...]], axis=1)
-    hits = jnp.where(gate == wanted, 1.0, 0.0)
-    guard = jnp.broadcast_to(guard_ref[...].astype(F32), (8, GATES)).astype(BF16)
-    keep = dot(guard, hits.astype(BF16))[0:1]
-    pick = (hits * keep).astype(BF16)
-    counts = dot_nt(jnp.full((8, 128), 0.5, BF16), pick)[0:1]
+        turned = turned_by(placed[1][b], b - 1)
+        send_wts[b] = (turned[:32] + pltpu.roll(turned[32:], 64, 1)).astype(BF16)
+
+    wide = lax.broadcasted_iota(jnp.int32, (PULSES, 128), 1)
+
+    def fill_lhs(b, sub, x):
+        lhs_re[pl.ds(b * 2 + sub, PULSES, stride=8), :] = x
+        lhs_im[pl.ds(b * 2 + sub, PULSES, stride=8), :] = jnp.where(
+            wide < 32, -pltpu.roll(x, 96, 1), pltpu.roll(x, 32, 1)
+        )
 
     fetches[4].wait()
     fetches[5].wait()
@@ -210,6 +232,16 @@
     wts_copy = remote(send_wts, got_wts, send_sem.at[0], recv_sem.at[0], (following, rng))
     wts_copy.start()
 
+    fetches[2].wait()
+    fetches[3].wait()
+    gate = lax.broadcasted_iota(jnp.int32, (GATES, 128), 0)
+    wanted = jnp.concatenate([idx_ref[...], idx_ref[...]], axis=1)
+    hits = jnp.where(gate == wanted, 1.0, 0.0)
+    guard = jnp.broadcast_to(guard_ref[...].astype(F32), (8, GATES)).astype(BF16)
+    keep = dot(guard, hits.astype(BF16))[0:1]
+    pick = (hits * keep).astype(BF16)
+    counts = dot_nt(jnp.full((8, 128), 0.5, BF16), pick)[0:1]
+
     left = lax.broadcasted_iota(jnp.int32, (CH, 128), 1) < TRAIN
 
     def gather_bins(step):
@@ -315,13 +347,20 @@
         return sums
 
     wts_copy.wait()
-    fill_lhs([got_wts[b].astype(F32) for b in range(3)])
+    for b in range(3):
+        packed = got_wts[b].astype(F32)
+        table = jnp.concatenate([packed, pltpu.roll(packed, 64, 1)], axis=0)
+        fill_lhs(b, 1, jnp.where(lax.rem(wide, 32) < HALO, table, 0.0))
+        fill_lhs(b, 0, jnp.where(lax.rem(wide, 32) < CH - HALO, pltpu.roll(table, 128 - HALO, 1), 0.0))
     for part, value in enumerate(filtered()):
         send_part[part] = value
     part_copy = remote(send_part, got_part, send_sem.at[1], recv_sem.at[1], (prev, rng))
     part_copy.start()
 
-    fill_lhs([turned_by(placed[0][b], b - 1) for b in range(3)])
+    for b in range(3):
+        turned = turned_by(placed[0][b], b - 1)
+        fill_lhs(b, 0, turned)
+        fill_lhs(b, 1, pltpu.roll(turned, 64, 1))
     own = filtered()
 
     norms = []
@@ -339,18 +378,20 @@
 
     low = lax.broadcasted_iota(jnp.int32, (SUB, 128), 1) < TRAIN
 
-    def arrange(step, carry):
-        rows = pl.multiple_of(step * (2 * HALO), 2 * HALO)
-        same = got_same[pl.ds(rows, 2 * HALO), :].astype(F32)
-        for u in range(2):
-            k = step * 2 + u
+    def arrange(first, width, step, carry):
+        begin = first + step * width
+        for u in range(width):
+            k = begin + u
             start = pl.multiple_of(k * EXT, 8)
+            if u % 2 == 0:
+                rows = pl.multiple_of(k * HALO, 2 * HALO)
+                same = got_same[pl.ds(rows, 2 * HALO), :].astype(F32)
             ext_a[pl.ds(start, CH), :] = train[rng * HALF + k].astype(F32)
-            ext_a[pl.ds(start + CH, HALO), :] = same[u * HALO : u * HALO + HALO]
+            ext_a[pl.ds(start + CH, HALO), :] = same[u % 2 * HALO : u % 2 * HALO + HALO]
             ext_b[pl.ds(start, CH), :] = got_train[k].astype(F32)
             ext_b[pl.ds(start + CH, HALO), :] = got_cross[k].astype(F32)[:HALO]
-        for u in range(2):
-            k = step * 2 + u
+        for u in range(width):
+            k = begin + u
             row = pl.multiple_of(k * SUB, SUB)
             for sub in range(2):
                 start = k * EXT + 16 * sub + off_ref[sub]
@@ -361,7 +402,7 @@
                     BF16
                 )
                 by_four = [
-                    jnp.concatenate([ext[pl.ds(start + a, 8, stride=4), :] for a in range(4)], axis=0)
+                    jnp.concatenate([ext[pl.ds(start + a, 8, stride=4), :] for a in range(4)], axis=0) * (1.0 / 128.0)
                     for ext in (ext_a, ext_b)
                 ]
                 lhs_cov[sub, pl.ds(row + 2 * SUB, SUB), :] = jnp.concatenate(by_four, axis=1).astype(BF16)
@@ -373,31 +414,6 @@
             right = jnp.concatenate([rhs_re[sub, pl.ds(row, 128), :], rhs_im[sub, pl.ds(row, 128), :]], axis=0)
             tiles[sub, pl.ds(g * 256, 256), :] = dot_nt(lhs_cov[sub, pl.ds(row, 256), :], right)
 
-    col = lax.broadcasted_iota(jnp.int32, (8, 128), 1)
-
-    def lay_out(g, carry):
-        here = pl.multiple_of(g * 256, 256)
-        for r in range(4):
-            for sub in range(2):
-                base = ((g * 4 + r) * 2 + sub) * ROWS
-                for part in range(2):
-                    lanes = slice(part * 128, part * 128 + 128)
-                    by = [[], [], [], []]
-                    for b in range(3):
-                        block = tiles[sub, pl.ds(here + (r + b + 2) * 32, 32), lanes]
-                        if r >= 2:
-                            after = tiles[sub, pl.ds(here + 256 + (r + b - 2) * 32, 32), lanes]
-                        for a in range(4):
-                            x = block[a * 8 : a * 8 + 8]
-                            if r >= 2:
-                                x = jnp.where(col >= r * 32, x, after[a * 8 : a * 8 + 8])
-                            shift = (3 * a - r) % 4 * 32
-                            by[a].append((pltpu.roll(x, shift, 1) if shift else x) * (1.0 / 128.0))
-                    for u, edge in enumerate((96, 64, 32)):
-                        row = jnp.concatenate([jnp.where(col < edge, by[u][b], by[u + 1][b]) for b in range(3)], axis=0)
-                        cov[pl.ds(base + 2 * u + part, 24, stride=6), :] = row
-        return carry
-
     def pass_on(piece):
         train_copy(piece).wait_recv()
 
@@ -412,11 +428,13 @@
         first, count = PIECES[piece]
         same_copy(piece).wait_recv()
         relay_copy(piece).wait_recv()
-        lax.fori_loop(first // 2, (first + count) // 2, arrange, 0)
+        width = 4 if count % 4 == 0 else 2
+        lax.fori_loop(0, count // width, functools.partial(arrange, first, width), 0)
         begin = ready[piece - 1] if piece else 0
         for g in range(begin, ready[piece]):
             tile(g)
-        lax.fori_loop(max(begin - 1, 0), ready[piece] - 1, lay_out, 0)
+        if ready[piece] - 1 <= HEAD:
+            lax.fori_loop(max(begin - 1, 0), ready[piece] - 1, functools.partial(lay_out, tiles, head, 0), 0)
 
     pass_on(0)
     cover(0)
@@ -438,11 +456,11 @@
 
 
     pass_on(1)
-    cover(1)
 
     collect(sum_a, n_a, 7, peer_a)
     sum_b[n_b - 1] = jnp.sum(sum_a[...], axis=0)
     spread(sum_b, n_b, 6, peer_b)
+    cover(1)
     pass_on(2)
     cover(2)
     pass_on(3)
@@ -465,15 +483,29 @@
     remote(train_span, got_cross, send_sem.at[5], cross_recv.at[0], (prev, rng)).wait_send()
 
 
-def hand_out(cov, matched, pmap, cov_out, matched_out, pmap_out, sem):
-    rows = cov.shape[0] // PARTS
-    parts = [(cov.at[pl.ds(i * rows, rows)], cov_out.at[pl.ds(i * rows, rows)]) for i in range(PARTS)]
-    pairs = (*parts, (matched, matched_out), (pmap, pmap_out))
+def hand_out(tiles, head, matched, pmap, cov_out, matched_out, pmap_out, cov, sem):
+    pairs = ((head, cov_out.at[pl.ds(0, HEAD * 8 * ROWS)]), (matched, matched_out), (pmap, pmap_out))
     copies = [pltpu.make_async_copy(src, dst, sem.at[i]) for i, (src, dst) in enumerate(pairs)]
     for copy in copies:
         copy.start()
+    def cov_copy(g):
+        source = pl.ds(pl.multiple_of((g - HEAD) * (8 * ROWS), 8 * ROWS), 8 * ROWS)
+        rows = pl.ds(pl.multiple_of(g * (8 * ROWS), 8 * ROWS), 8 * ROWS)
+        return pltpu.make_async_copy(cov.at[source], cov_out.at[rows], sem.at[3 + g - HEAD])
+
+    def chunk(g, carry):
+        lay_out(tiles, cov, HEAD, g, carry)
+        cov_copy(g).start()
+        return carry
+
+    def chunk_done(g, carry):
+        cov_copy(g).wait()
+        return carry
+
+    lax.fori_loop(HEAD, HALF // 4, chunk, 0)
     for copy in copies:
         copy.wait()
+    lax.fori_loop(HEAD, HALF // 4, chunk_done, 0)
 
 
 def local(sizes, radar_cube, offsets, train_index, guard_mask, weights):
@@ -484,16 +516,16 @@
     vmem = pl.BlockSpec(memory_space=pltpu.VMEM)
     hbm = pl.BlockSpec(memory_space=pltpu.HBM)
     rows = HALF * 2 * ROWS
-    shapes = (
-        jax.ShapeDtypeStruct((rows, 128), F32),
-        jax.ShapeDtypeStruct((2, PULSES, GATES), F32),
-        jax.ShapeDtypeStruct((2, PULSES, GATES), F32),
-    )
+    maps = (jax.ShapeDtypeStruct((2, PULSES, GATES), F32),) * 2
     held = pl.pallas_call(
         functools.partial(kernel, sizes),
-        out_shape=shapes,
+        out_shape=(
+            jax.ShapeDtypeStruct((2, (HALF // 4 + 1) * 256, 256), F32),
+            jax.ShapeDtypeStruct((HEAD * 8 * ROWS, 128), F32),
+            *maps,
+        ),
         in_specs=[hbm] * 6,
-        out_specs=(vmem, vmem, vmem),
+        out_specs=(vmem, vmem, vmem, vmem),
         scratch_shapes=[
             pltpu.SMEM((2,), jnp.int32),
             pltpu.VMEM((2, CH, PULSES, GATES), BF16),
@@ -508,8 +540,8 @@
             pltpu.VMEM((BINS, CH, 128), BF16),
             pltpu.VMEM((BINS * HALO, 128), BF16),
             pltpu.VMEM((BINS, CH, 128), BF16),
-            pltpu.VMEM((3, PULSES, 128), BF16),
-            pltpu.VMEM((3, PULSES, 128), BF16),
+            pltpu.VMEM((3, PULSES // 2, 128), BF16),
+            pltpu.VMEM((3, PULSES // 2, 128), BF16),
             pltpu.VMEM((PULSES * 8, 128), F32),
             pltpu.VMEM((PULSES * 8, 128), F32),
             pltpu.VMEM((PULSES * 8, 128), F32),
@@ -525,7 +557,6 @@
             pltpu.VMEM((2, (BINS + 2) * SUB, 256), BF16),
             pltpu.VMEM((2, (BINS + 2) * SUB, 256), BF16),
             pltpu.VMEM((2, (BINS + 6) * SUB, 256), BF16),
-            pltpu.VMEM((2, (HALF // 4 + 1) * 256, 256), F32),
             dma((6,)),
             dma((8,)),
             dma((5,)),
@@ -551,11 +582,11 @@
     )
     cov, matched, pmap = pl.pallas_call(
         hand_out,
-        out_shape=shapes,
-        in_specs=[vmem] * 3,
+        out_shape=(jax.ShapeDtypeStruct((rows, 128), F32), *maps),
+        in_specs=[vmem] * 4,
         out_specs=(hbm, hbm, hbm),
-        scratch_shapes=[dma((PARTS + 2,))],
-        compiler_params=pltpu.CompilerParams(vmem_limit_bytes=1024 * 1024),
+        scratch_shapes=[pltpu.VMEM((rows - HEAD * 8 * ROWS, 128), F32), dma((3 + HALF // 4 - HEAD,))],
+        compiler_params=pltpu.CompilerParams(vmem_limit_bytes=8 * 1024 * 1024),
     )(*held)
     cov = cov.reshape(HALF, 2, ROWS // 2, 2, 128).transpose(0, 1, 3, 2, 4).reshape(HALF, 2, 2, ROWS * 64)
     return cov, matched, pmap

time: 33.6 us -> 33.5 us (level)
  no operation moved by 1% of the time
where the time goes in v3:
time: 33.5 us; the launch traced here: 33.4 us
  Pallas kernels  32.8 us (98%)
  between operations  0.64 us (2%)
    pallas_call x1, Pallas kernels, local(): pl.pallas_call(functools.partial(kernel, sizes), out_shape=(jax.ShapeDtyp...  30.5 us
    pallas_call x1, Pallas kernels, local(): pl.pallas_call(hand_out, out_shape=(jax.ShapeDtypeStruct((rows, 128), F32...  2.29 us

profile of v3, /device:TPU:1, one launch (start us, length us, event | category | flops | bytes accessed | tf_op | source)
XLA Modules:
  0.0 33.4 jit_solution(10241045665447299520)
XLA Ops:
  0.6 30.5 %shard_map.85 = (f32[2,2304,256]{2,1,0:T(8,128)S(1)}, f32[3456,128]{1,0:T(8,128)S(1)}, f32[2,64,128]{2,1,0:T(8,128)S(1)}, f32[2,64,128]{2,1,0:T(8,128)S(1)}) custom-call(s32[2]{0:T(128)} %off_hbm.1, bf16[2,32,64,128]{3,2,1,0:T(8,128)(2,1)} %cube_hbm.1, s32[1,64]{1,0:T(1,128)} %bitcast.7, s32[1,128]{1,0:T(1,128)} %bitcast.8, bf16[2,2,64,96]{3,2,1,0:T(8,128)(2,1)} %wts_hbm.1, ...), custom_call_target="tpu_custom_call" | custom-call | tf_op jit(solution)/shard_map/pallas_call | solution.py:520
  31.1 2.3 %shard_map.86 = (f32[9216,128]{1,0:T(8,128)}, f32[2,64,128]{2,1,0:T(8,128)}, f32[2,64,128]{2,1,0:T(8,128)}) custom-call(f32[2,2304,256]{2,1,0:T(8,128)S(1)} %get-tuple-element.10.tiles, f32[3456,128]{1,0:T(8,128)S(1)} %get-tuple-element.11.head, f32[2,64,128]{2,1,0:T(8,128)S(1)} %get-tuple-element.12.matched, f32[2,64,128]{2,1,0:T(8,128)S(1)} %get-tuple-element.13.pmap), custom_call_target="tpu_custom_call" | custom-call | tf_op jit(solution)/shard_map/pallas_call | solution.py:583

commit v4 on v3

--- a/solution.py
+++ b/solution.py
@@ -436,8 +436,11 @@
         if ready[piece] - 1 <= HEAD:
             lax.fori_loop(max(begin - 1, 0), ready[piece] - 1, functools.partial(lay_out, tiles, head, 0), 0)
 
-    pass_on(0)
-    cover(0)
+    @pl.when(core == 1)
+    def _():
+        pass_on(0)
+        cover(0)
+
     part_copy.wait()
     powers = []
     for sub in range(2):
@@ -447,6 +450,12 @@
     sum_a[n_a - 1] = jnp.sum(powers[0] + powers[1], axis=0, keepdims=True)
 
     spread(sum_a, n_a, 7, peer_a)
+
+    @pl.when(core == 0)
+    def _():
+        pass_on(0)
+        cover(0)
+
     for piece in range(1, len(PIECES)):
         send_piece(piece)
     quads = [jnp.sum(p * counts, axis=1, keepdims=True) for p in powers]

time: 33.5 us -> 33.5 us (level)
  no operation moved by 1% of the time
where the time goes in v4:
time: 33.5 us; the launch traced here: 33.4 us
  Pallas kernels  32.8 us (98%)
  between operations  0.64 us (2%)
    pallas_call x1, Pallas kernels, local(): pl.pallas_call(functools.partial(kernel, sizes), out_shape=(jax.ShapeDtyp...  30.5 us
    pallas_call x1, Pallas kernels, local(): pl.pallas_call(hand_out, out_shape=(jax.ShapeDtypeStruct((rows, 128), F32...  2.29 us

profile of v4, /device:TPU:1, one launch (start us, length us, event | category | flops | bytes accessed | tf_op | source)
XLA Modules:
  0.0 33.4 jit_solution(14539014951099052017)
XLA Ops:
  0.6 30.5 %shard_map.85 = (f32[2,2304,256]{2,1,0:T(8,128)S(1)}, f32[3456,128]{1,0:T(8,128)S(1)}, f32[2,64,128]{2,1,0:T(8,128)S(1)}, f32[2,64,128]{2,1,0:T(8,128)S(1)}) custom-call(s32[2]{0:T(128)} %off_hbm.1, bf16[2,32,64,128]{3,2,1,0:T(8,128)(2,1)} %cube_hbm.1, s32[1,64]{1,0:T(1,128)} %bitcast.7, s32[1,128]{1,0:T(1,128)} %bitcast.8, bf16[2,2,64,96]{3,2,1,0:T(8,128)(2,1)} %wts_hbm.1, ...), custom_call_target="tpu_custom_call" | custom-call | tf_op jit(solution)/shard_map/pallas_call | solution.py:529
  31.1 2.3 %shard_map.86 = (f32[9216,128]{1,0:T(8,128)}, f32[2,64,128]{2,1,0:T(8,128)}, f32[2,64,128]{2,1,0:T(8,128)}) custom-call(f32[2,2304,256]{2,1,0:T(8,128)S(1)} %get-tuple-element.10.tiles, f32[3456,128]{1,0:T(8,128)S(1)} %get-tuple-element.11.head, f32[2,64,128]{2,1,0:T(8,128)S(1)} %get-tuple-element.12.matched, f32[2,64,128]{2,1,0:T(8,128)S(1)} %get-tuple-element.13.pmap), custom_call_target="tpu_custom_call" | custom-call | tf_op jit(solution)/shard_map/pallas_call | solution.py:592
